TPU v7x, 32 devices: a whole 2x2x4 slice. The times are simulated.
32 devices in a mesh: dp: 8 (over z, x), seq: 4 (over y, core).
Axes of the slice: x: 2, y: 2, z: 4, core: 2. Of those that a mesh axis runs over, the one named last changes fastest.
Arguments:
- tokens: bfloat16 [16, 1536, 768], P('dp', 'seq'), may hold values from -6 to 6
- cube_lengths: int32 [16], P('dp'), may hold values from 864 to 1536, as said below
- key_mask: int32 [16, 1536], P('dp'), may hold values from 0 to 1, as said below
- cotangent: bfloat16 [16, 1536, 768], P('dp', 'seq'), may hold values from -6 to 6
- norm_gain: bfloat16 [768], P(('dp', 'seq')), may hold values from 0.099609375 to 1.8984375
- norm_shift: bfloat16 [768], P(('dp', 'seq')), may hold values from -3 to 3
- proj_weight: bfloat16 [768, 2304], P(('dp', 'seq')), may hold values from -0.21875 to 0.21875
- query_bias: bfloat16 [768], P(('dp', 'seq')), may hold values from -3 to 3
- value_bias: bfloat16 [768], P(('dp', 'seq')), may hold values from -0.29882812 to 0.29882812
- merge_weight: bfloat16 [768, 768], P(('dp', 'seq')), may hold values from -4 to 4
- merge_bias: bfloat16 [768], P(('dp', 'seq')), may hold values from -2 to 2
- mlp_gain: bfloat16 [768], P(('dp', 'seq')), may hold values from 0.099609375 to 1.8984375
- mlp_shift: bfloat16 [768], P(('dp', 'seq')), may hold values from -3 to 3
- expand_weight: bfloat16 [768, 3072], P(('dp', 'seq')), may hold values from -0.21875 to 0.21875
- expand_bias: bfloat16 [3072], P(('dp', 'seq')), may hold values from -3 to 3
- reduce_weight: bfloat16 [3072, 768], P(('dp', 'seq')), may hold values from -0.109375 to 0.109375
- reduce_bias: bfloat16 [768], P(('dp', 'seq')), may hold values from -2 to 2
Outputs:
- activations: bfloat16 [16, 1536, 768], P('dp', 'seq')
- input_grad: float32 [16, 1536, 768], P('dp', 'seq')
- norm_gain_grad: float32 [768], P(('dp', 'seq'))
- norm_shift_grad: float32 [768], P(('dp', 'seq'))
- proj_weight_grad: float32 [768, 2304], P(('dp', 'seq'))
- query_bias_grad: float32 [768], P(('dp', 'seq'))
- value_bias_grad: float32 [768], P(('dp', 'seq'))
- merge_weight_grad: float32 [768, 768], P(('dp', 'seq'))
- merge_bias_grad: float32 [768], P(('dp', 'seq'))
- mlp_gain_grad: float32 [768], P(('dp', 'seq'))
- mlp_shift_grad: float32 [768], P(('dp', 'seq'))
- expand_weight_grad: float32 [768, 3072], P(('dp', 'seq'))
- expand_bias_grad: float32 [3072], P(('dp', 'seq'))
- reduce_weight_grad: float32 [3072, 768], P(('dp', 'seq'))
- reduce_bias_grad: float32 [768], P(('dp', 'seq'))
Inputs may be any that keep to these rules, and one draw needn't show every extreme that they name: `cube_lengths`: each cube holds 1536 or 864 tokens and its remaining slots are padding; cube 0 holds 1536 and cube 1 holds 864. `key_mask`: slot 0 of every cube is 1.
All inputs are finite; a program needn't handle non-finite values.
Results may differ from a plain program's by a relative error of at most 0.012.
Values may be sent and summed in bfloat16 or wider, within the bound.
A program may use at most 192 MiB of HBM per device.

v0:
```python
import jax
import jax.numpy as jnp
from jax import lax
from jax.sharding import PartitionSpec as P

HD = 64


EPSILON = 1e-06


def norm_rows(v, gain, shift):
    mean = jnp.mean(v, axis=-1, keepdims=True)
    center = v - mean
    spread = jnp.mean(center * center, axis=-1, keepdims=True)
    return center * lax.rsqrt(spread + EPSILON) * gain + shift


def gelu_exact(v):
    return jax.nn.gelu(v, approximate=False)


def column(table, start):
    return lax.dynamic_slice_in_dim(table, start, HD, 2)


def shards(
    tokens,
    cube_lengths,
    key_mask,
    cotangent,
    norm_gain,
    norm_shift,
    proj_weight,
    query_bias,
    value_bias,
    merge_weight,
    merge_bias,
    mlp_gain,
    mlp_shift,
    expand_weight,
    expand_bias,
    reduce_weight,
    reduce_bias,
):
    gathered = (
        lax.all_gather(norm_gain, ("dp", "seq"), axis=0, tiled=True),
        lax.all_gather(norm_shift, ("dp", "seq"), axis=0, tiled=True),
        lax.all_gather(proj_weight, ("dp", "seq"), axis=0, tiled=True),
        lax.all_gather(query_bias, ("dp", "seq"), axis=0, tiled=True),
        lax.all_gather(value_bias, ("dp", "seq"), axis=0, tiled=True),
        lax.all_gather(merge_weight, ("dp", "seq"), axis=0, tiled=True),
        lax.all_gather(merge_bias, ("dp", "seq"), axis=0, tiled=True),
        lax.all_gather(mlp_gain, ("dp", "seq"), axis=0, tiled=True),
        lax.all_gather(mlp_shift, ("dp", "seq"), axis=0, tiled=True),
        lax.all_gather(expand_weight, ("dp", "seq"), axis=0, tiled=True),
        lax.all_gather(expand_bias, ("dp", "seq"), axis=0, tiled=True),
        lax.all_gather(reduce_weight, ("dp", "seq"), axis=0, tiled=True),
        lax.all_gather(reduce_bias, ("dp", "seq"), axis=0, tiled=True),
    )
    (
        gain_first,
        shift_first,
        proj_full,
        query_add,
        value_add,
        merge_full,
        merge_add,
        gain_second,
        shift_second,
        expand_full,
        expand_add,
        reduce_full,
        reduce_add,
    ) = gathered
    slots, local_len, width = tokens.shape
    full_len = key_mask.shape[1]
    heads = width // HD
    scale = HD ** (-0.5)
    rows = slots * local_len
    f32 = jnp.float32
    bf16 = jnp.bfloat16
    resid = tokens.reshape(rows, width).astype(f32)
    first_f, first_pull = jax.vjp(norm_rows, resid, gain_first.astype(f32), shift_first.astype(f32))
    first = first_f.astype(bf16)
    packed = jnp.dot(first, proj_full, preferred_element_type=f32)
    query = (
        (packed[:, :width] + query_add.astype(f32)).astype(bf16).reshape(slots, local_len, width)
    )
    keys = packed[:, width : 2 * width].astype(bf16).reshape(slots, local_len, width)
    values = (
        (packed[:, 2 * width :] + value_add.astype(f32))
        .astype(bf16)
        .reshape(slots, local_len, width)
    )
    keys_all, values_all = (
        lax.all_gather(keys, "seq", axis=1, tiled=True),
        lax.all_gather(values, "seq", axis=1, tiled=True),
    )
    positions = lax.broadcasted_iota(jnp.int32, (slots, full_len), 1)
    valid = (key_mask > 0) & (positions < cube_lengths[:, None])

    def scores_of(query_h, keys_h, usable):
        raw = jnp.einsum("sqd,skd->sqk", query_h, keys_h, preferred_element_type=f32) * scale
        return jnp.where(usable[:, None, :], raw, -1e30)

    def forward_head(carry, head):
        scores = scores_of(column(query, head * HD), column(keys_all, head * HD), valid)
        top = jnp.max(scores, axis=-1, keepdims=True)
        expo = jnp.exp(scores - top)
        total = jnp.sum(expo, axis=-1, keepdims=True)
        probs = (expo / total).astype(bf16)
        result = jnp.einsum(
            "sqk,skd->sqd", probs, column(values_all, head * HD), preferred_element_type=f32
        )
        return (carry, (result, top[..., 0] + jnp.log(total[..., 0])))

    _, (attn_heads, logsum) = lax.scan(forward_head, 0, jnp.arange(heads))
    attn = attn_heads.transpose(1, 2, 0, 3).reshape(rows, width).astype(bf16)
    middle = resid + jnp.dot(attn, merge_full, preferred_element_type=f32) + merge_add.astype(f32)
    second_f, second_pull = jax.vjp(
        norm_rows, middle, gain_second.astype(f32), shift_second.astype(f32)
    )
    second = second_f.astype(bf16)
    hidden = jnp.dot(second, expand_full, preferred_element_type=f32) + expand_add.astype(f32)
    act_f, gelu_pull = jax.vjp(gelu_exact, hidden)
    act = act_f.astype(bf16)
    output = middle + jnp.dot(act, reduce_full, preferred_element_type=f32) + reduce_add.astype(f32)
    activations = output.astype(bf16).reshape(slots, local_len, width)
    backward_set = (
        lax.all_gather(norm_gain, ("dp", "seq"), axis=0, tiled=True),
        lax.all_gather(norm_shift, ("dp", "seq"), axis=0, tiled=True),
        lax.all_gather(proj_weight, ("dp", "seq"), axis=0, tiled=True),
        lax.all_gather(query_bias, ("dp", "seq"), axis=0, tiled=True),
        lax.all_gather(value_bias, ("dp", "seq"), axis=0, tiled=True),
        lax.all_gather(merge_weight, ("dp", "seq"), axis=0, tiled=True),
        lax.all_gather(merge_bias, ("dp", "seq"), axis=0, tiled=True),
        lax.all_gather(mlp_gain, ("dp", "seq"), axis=0, tiled=True),
        lax.all_gather(mlp_shift, ("dp", "seq"), axis=0, tiled=True),
        lax.all_gather(expand_weight, ("dp", "seq"), axis=0, tiled=True),
        lax.all_gather(expand_bias, ("dp", "seq"), axis=0, tiled=True),
        lax.all_gather(reduce_weight, ("dp", "seq"), axis=0, tiled=True),
        lax.all_gather(reduce_bias, ("dp", "seq"), axis=0, tiled=True),
    )
    proj_back = backward_set[2]
    merge_back = backward_set[5]
    expand_back = backward_set[9]
    reduce_back = backward_set[11]
    upstream = cotangent.reshape(rows, width)
    upstream_f = upstream.astype(f32)
    reduce_bias_grad = jnp.sum(upstream_f, axis=0)
    reduce_weight_grad = jnp.einsum("rf,rd->fd", act, upstream, preferred_element_type=f32)
    act_grad = jnp.einsum("rd,fd->rf", upstream, reduce_back, preferred_element_type=f32)
    hidden_grad = gelu_pull(act_grad)[0].astype(bf16)
    expand_bias_grad = jnp.sum(hidden_grad.astype(f32), axis=0)
    expand_weight_grad = jnp.einsum("rd,rf->df", second, hidden_grad, preferred_element_type=f32)
    second_grad = jnp.einsum("rf,df->rd", hidden_grad, expand_back, preferred_element_type=f32)
    middle_norm, mlp_gain_grad, mlp_shift_grad = second_pull(second_grad)
    middle_grad = upstream_f + middle_norm
    merged_grad = middle_grad.astype(bf16)
    merge_bias_grad = jnp.sum(merged_grad.astype(f32), axis=0)
    merge_weight_grad = jnp.einsum("rd,re->de", attn, merged_grad, preferred_element_type=f32)
    attn_grad = jnp.einsum("re,de->rd", merged_grad, merge_back, preferred_element_type=f32)
    attn_grad = attn_grad.astype(bf16).reshape(slots, local_len, width)

    def grad_terms(query_h, keys_h, values_h, grad_h, lse, usable):
        scores = scores_of(query_h, keys_h, usable)
        probs = jnp.exp(scores - lse[..., None])
        prob_grad = jnp.einsum("sqd,skd->sqk", grad_h, values_h, preferred_element_type=f32)
        delta = jnp.sum(probs * prob_grad, axis=-1)
        score_grad = (probs * (prob_grad - delta[..., None]) * scale).astype(bf16)
        return (probs, score_grad, delta)

    def backward_head(carry, item):
        head, lse = item
        query_h = column(query, head * HD)
        keys_h = column(keys_all, head * HD)
        grad_h = column(attn_grad, head * HD)
        probs, score_grad, delta = grad_terms(
            query_h, keys_h, column(values_all, head * HD), grad_h, lse, valid
        )
        query_part = jnp.einsum("sqk,skd->sqd", score_grad, keys_h, preferred_element_type=f32)
        key_part = jnp.einsum("sqk,sqd->skd", score_grad, query_h, preferred_element_type=f32)
        value_part = jnp.einsum(
            "sqk,sqd->skd", probs.astype(bf16), grad_h, preferred_element_type=f32
        )
        return (carry, (query_part, key_part, value_part))

    _, (query_parts, key_parts, value_parts) = lax.scan(
        backward_head, 0, (jnp.arange(heads), logsum)
    )
    key_whole = key_parts.transpose(1, 2, 0, 3).reshape(slots, full_len, width)
    value_whole = value_parts.transpose(1, 2, 0, 3).reshape(slots, full_len, width)
    key_sum, value_sum = (
        lax.psum_scatter(
            key_whole.astype(jnp.bfloat16), "seq", scatter_dimension=1, tiled=True
        ).astype(jnp.float32),
        lax.psum_scatter(
            value_whole.astype(jnp.bfloat16), "seq", scatter_dimension=1, tiled=True
        ).astype(jnp.float32),
    )
    key_grad = key_sum.reshape(rows, width).astype(bf16)
    value_grad = value_sum.reshape(rows, width).astype(bf16)
    query_grad = query_parts.transpose(1, 2, 0, 3).reshape(rows, width).astype(bf16)
    query_bias_grad = jnp.sum(query_grad.astype(f32), axis=0)
    value_bias_grad = jnp.sum(value_grad.astype(f32), axis=0)
    packed_grad = jnp.concatenate([query_grad, key_grad, value_grad], axis=1)
    proj_weight_grad = jnp.einsum("rd,re->de", first, packed_grad, preferred_element_type=f32)
    first_grad = jnp.einsum("re,de->rd", packed_grad, proj_back, preferred_element_type=f32)
    resid_norm, norm_gain_grad, norm_shift_grad = first_pull(first_grad)
    input_grad = (middle_grad + resid_norm).reshape(slots, local_len, width)
    summed = (
        lax.psum_scatter(norm_gain_grad, ("dp", "seq"), scatter_dimension=0, tiled=True),
        lax.psum_scatter(norm_shift_grad, ("dp", "seq"), scatter_dimension=0, tiled=True),
        lax.psum_scatter(proj_weight_grad, ("dp", "seq"), scatter_dimension=0, tiled=True),
        lax.psum_scatter(query_bias_grad, ("dp", "seq"), scatter_dimension=0, tiled=True),
        lax.psum_scatter(value_bias_grad, ("dp", "seq"), scatter_dimension=0, tiled=True),
        lax.psum_scatter(merge_weight_grad, ("dp", "seq"), scatter_dimension=0, tiled=True),
        lax.psum_scatter(merge_bias_grad, ("dp", "seq"), scatter_dimension=0, tiled=True),
        lax.psum_scatter(mlp_gain_grad, ("dp", "seq"), scatter_dimension=0, tiled=True),
        lax.psum_scatter(mlp_shift_grad, ("dp", "seq"), scatter_dimension=0, tiled=True),
        lax.psum_scatter(expand_weight_grad, ("dp", "seq"), scatter_dimension=0, tiled=True),
        lax.psum_scatter(expand_bias_grad, ("dp", "seq"), scatter_dimension=0, tiled=True),
        lax.psum_scatter(reduce_weight_grad, ("dp", "seq"), scatter_dimension=0, tiled=True),
        lax.psum_scatter(reduce_bias_grad, ("dp", "seq"), scatter_dimension=0, tiled=True),
    )
    return (activations, input_grad) + tuple(summed)


def solution(mesh):
    in_specs = (
        P("dp", "seq", None),
        P("dp"),
        P("dp", None),
        P("dp", "seq", None),
        P(("dp", "seq")),
        P(("dp", "seq")),
        P(("dp", "seq"), None),
        P(("dp", "seq")),
        P(("dp", "seq")),
        P(("dp", "seq"), None),
        P(("dp", "seq")),
        P(("dp", "seq")),
        P(("dp", "seq")),
        P(("dp", "seq"), None),
        P(("dp", "seq")),
        P(("dp", "seq"), None),
        P(("dp", "seq")),
    )
    out_specs = (
        P("dp", "seq", None),
        P("dp", "seq", None),
        P(("dp", "seq")),
        P(("dp", "seq")),
        P(("dp", "seq"), None),
        P(("dp", "seq")),
        P(("dp", "seq")),
        P(("dp", "seq"), None),
        P(("dp", "seq")),
        P(("dp", "seq")),
        P(("dp", "seq")),
        P(("dp", "seq"), None),
        P(("dp", "seq")),
        P(("dp", "seq"), None),
        P(("dp", "seq")),
    )
    return jax.shard_map(shards, mesh=mesh, in_specs=in_specs, out_specs=out_specs, check_vma=False)
```

profile of v0, /device:TPU:0, one launch (start us, length us, event | category | flops | bytes accessed | tf_op | source)
XLA Modules:
  0.0 1392.1 jit_solution(426558043030277730)
XLA Ops:
  15.5 42.9 %all-reduce.19 = (bf16[768]{0:T(1024)(128)(2,1)S(1)}, bf16[768]{0:T(1024)(128)(2,1)S(1)}, bf16[768]{0:T(1024)(128)(2,1)S(1)}, bf16[768]{0:T(1024)(128)(2,1)S(1)}...) all-reduce(bf16[768]{0:T(1024)(128)(2,1)S(1)} %dynamic-update-slice, ...), channel_id=1, replica_groups=mesh['dp'=8,'seq'=4] {'dp','seq'}, use_global_device_ids=true, to_apply=%add.1 | all-reduce | flops 9216 | bytes 36864
  64.7 9.0 all-gather.7.cloned.1.call-done
  73.7 4.9 fusion.86
  91.5 27.9 %all-gather.9.cloned.1.call-done = bf16[2,1536,768]{1,2,0:T(8,128)(2,1)} async-done(((bf16[2,384,768]{1,2,0:T(8,128)(2,1)}), bf16[2,1536,768]{1,2,0:T(8,128)(2,1)}) %all-gather.9.cloned.1.call-update) | async-done | bytes 4718608 | tf_op jit(solution)/shard_map/all_gather | solution.py:97
  119.4 39.5 %all-gather.11.cloned.1.call-done = bf16[2,1536,768]{1,2,0:T(8,128)(2,1)} async-done(((bf16[2,384,768]{1,2,0:T(8,128)(2,1)}), bf16[2,1536,768]{1,2,0:T(8,128)(2,1)}) %all-gather.11.cloned.1.call-update) | async-done | bytes 4718608 | tf_op jit(solution)/shard_map/all_gather | solution.py:98
  159.1 94.0 %while.26 = (s32[]{:T(128)}, bf16[12,2,384,64]{2,3,1,0:T(8,128)(2,1)S(1)}, f32[12,2,384]{2,1,0:T(2,128)}, pred[2,1536]{1,0:T(4,128)(4,1)}, s32[12]{0:T(128)S(1)}...) while((s32[]{:T(128)}, ...), condition=%wide.region_5.6_spmd, body=%wide.region_2.5_spmd.sunk | while | flops 316144896 | bytes 15278275 | solution.py:118
  260.8 20.4 %all-gather.15.cloned.1.call-done = bf16[768,3072]{1,0:T(8,128)(2,1)} async-done(((bf16[24,3072]{1,0:T(8,128)(2,1)}), bf16[768,3072]{1,0:T(8,128)(2,1)}) %all-gather.15.cloned.1.call-update) | async-done | bytes 4718608 | tf_op jit(solution)/shard_map/all_gather | solution.py:56
  281.2 8.7 fusion.80
  289.9 55.9 %all-gather.17.cloned.1.call-done = bf16[3072,768]{1,0:T(8,128)(2,1)} async-done(((bf16[96,768]{1,0:T(8,128)(2,1)}), bf16[3072,768]{1,0:T(8,128)(2,1)}) %all-gather.17.cloned.1.call-update) | async-done | bytes 4718608 | tf_op jit(solution)/shard_map/all_gather | solution.py:58
  345.9 29.9 %convert_reduce_fusion = (f32[3072]{0:T(1024)}, bf16[768,3072]{1,0:T(8,128)(2,1)S(1)}, f32[768,3072]{1,0:T(8,128)}) fusion(f32[768,3072]{1,0:T(8,128)} %fusion.80, f32[3072]{0:T(1024)} %convert_element_type.161, bf16[768,768]{1,0:T(8,128)(2,1)S(1)} %bitcast.151, bf16[3072,768]{1,0:T(8,128)(2,1)} %all-gather.17.cloned.1.call-done), kind=kOutput, calls=%fused_computation.53 | convolution fusion | flops 3800822784 | bytes 29515776 | tf_op jit(solution)/shard_map/rd,fd->rf/dot_general | solution.py:153
  375.8 4.8 multiply_reduce_fusion.1
  388.4 367.7 %while.27 = (s32[]{:T(128)}, bf16[12,2,384,64]{2,3,1,0:T(8,128)(2,1)S(1)}, bf16[12,2,1536,64]{2,3,0,1:T(8,128)(2,1)}, bf16[12,2,1536,64]{2,3,0,1:T(8,128)(2,1)},...) while((s32[]{:T(128)}, ...), condition=%wide.region_12.13_spmd, body=%wide.region_10.12_spmd.sunk | while | flops 771494400 | bytes 55264488 | solution.py:189
  391.2 4.3 subtract_exponential_fusion.3
  399.4 7.6 fusion.145
  407.1 8.5 fusion.146
  421.8 4.3 subtract_exponential_fusion.3
  430.1 7.6 fusion.145
  437.7 8.5 fusion.146
  452.4 4.3 subtract_exponential_fusion.3
  460.7 7.6 fusion.145
  468.3 8.4 fusion.146
  483.0 4.3 subtract_exponential_fusion.3
  491.3 7.7 fusion.145
  498.9 8.4 fusion.146
  513.6 4.3 subtract_exponential_fusion.3
  521.9 7.6 fusion.145
  529.5 8.5 fusion.146
  544.3 4.3 subtract_exponential_fusion.3
  552.5 7.6 fusion.145
  560.1 8.4 fusion.146
  574.9 4.3 subtract_exponential_fusion.3
  583.1 7.6 fusion.145
  590.7 8.5 fusion.146
  605.5 4.3 subtract_exponential_fusion.3
  613.8 7.6 fusion.145
  621.4 8.5 fusion.146
  636.2 4.3 subtract_exponential_fusion.3
  644.4 7.6 fusion.145
  652.0 8.5 fusion.146
  666.8 4.3 subtract_exponential_fusion.3
  675.0 7.6 fusion.145
  682.7 8.5 fusion.146
  697.4 4.3 subtract_exponential_fusion.3
  705.7 7.6 fusion.145
  713.3 8.5 fusion.146
  728.0 4.3 subtract_exponential_fusion.3
  736.3 7.6 fusion.145
  743.9 8.5 fusion.146
  756.1 12.7 copy.59
  768.8 5.4 copy.88
  774.3 12.8 copy.61
  787.2 5.6 copy.90
  797.1 10.9 fusion.79
  808.6 11.0 multiply_convert_fusion.1
  819.7 10.6 fusion.89
  842.0 29.3 %reduce-scatter.21.cloned.1.call-done = bf16[384,1536]{1,0:T(8,128)(2,1)} async-done(((bf16[1536,1536]{1,0:T(8,128)(2,1)}), bf16[384,1536]{1,0:T(8,128)(2,1)}) %reduce-scatter.21.cloned.1.call-update) | async-done | bytes 1179664
  882.6 7.1 fusion.87
  893.4 9.4 add_convert_fusion.1
  902.8 5.1 copy.62
  910.1 7.2 fusion.81
  920.4 41.6 %all-reduce.18 = (f32[768]{0:T(1024)}, f32[768]{0:T(1024)}, f32[768]{0:T(1024)}, f32[768]{0:T(1024)}, f32[768]{0:T(1024)}, /*index=5*/f32[768]{0:T(1024)}, f32[768]{0:T(1024)}, f32[3072]{0:T(1024)}, f32[768]{0:T(1024)}) all-reduce(f32[768]{0:T(1024)} %get-tuple-element.181, ...), channel_id=4, replica_groups=mesh['dp'=8,'seq'=4] {'dp','seq'}, use_global_device_ids=true, to_apply=%region_18.19.clone | all-reduce | flops 9216 | bytes 73728
  977.8 140.8 %reduce-scatter.15.cloned.1.call-done = f32[24,3072]{1,0:T(8,128)} async-done(((f32[768,3072]{1,0:T(8,128)}), f32[24,3072]{1,0:T(8,128)}) %reduce-scatter.15.cloned.1.call-update) | async-done | bytes 294928 | tf_op jit(solution)/shard_map/reduce_scatter | solution.py:222
  1118.6 141.6 %reduce-scatter.17.cloned.1.call-done = f32[96,768]{1,0:T(8,128)} async-done(((f32[3072,768]{1,0:T(8,128)}), f32[96,768]{1,0:T(8,128)}) %reduce-scatter.17.cloned.1.call-update) | async-done | bytes 294928 | tf_op jit(solution)/shard_map/reduce_scatter | solution.py:224
  1260.2 124.5 %reduce-scatter.11.cloned.1.call-done = f32[24,2304]{1,0:T(8,128)} async-done(((f32[768,2304]{1,0:T(8,128)}), f32[24,2304]{1,0:T(8,128)}) %reduce-scatter.11.cloned.1.call-update) | async-done | bytes 221200 | tf_op jit(solution)/shard_map/reduce_scatter | solution.py:215
  (290 shorter events, 296.6 us)
Async XLA Ops:
  7.2 66.5 %all-gather.7.cloned.1.call-start = ((), (), s32[]{:S(2)}) async-start(), calls=%async_computation.6 | async-start | bytes 3649536 | tf_op jit(solution)/shard_map/all_gather | solution.py:49
  7.9 111.5 %all-gather.9.cloned.1.call-start = ((), (), s32[]{:S(2)}) async-start(), calls=%async_computation.7 | async-start | bytes 5898240 | tf_op jit(solution)/shard_map/all_gather | solution.py:97
  58.4 20.2 %copy-start.18 = (f32[768]{0:T(1024)}, f32[768]{0:T(1024)S(1)}, u32[]{:S(2)}) copy-start(f32[768]{0:T(1024)S(1)} %convert_element_type.147) | copy-start | bytes 9220
  59.9 18.7 %copy-start.16 = (f32[768]{0:T(1024)}, f32[768]{0:T(1024)S(1)}, u32[]{:S(2)}) copy-start(f32[768]{0:T(1024)S(1)} %div.47) | copy-start | bytes 9220
  61.7 0.6 copy-start.26
  62.3 0.6 copy-start.20
  64.7 9.0 copy-start.11
  78.6 2.9 copy-start.8
  83.1 75.9 %all-gather.11.cloned.1.call-start = ((), (), s32[]{:S(2)}) async-start(), calls=%async_computation.8 | async-start | bytes 5898240 | tf_op jit(solution)/shard_map/all_gather | solution.py:98
  85.9 4.1 copy-start.28
  86.0 4.1 copy-start.30
  87.4 169.2 %all-gather.13.cloned.1.call-start = ((), (), s32[]{:S(2)}) async-start(), calls=%async_computation.9 | async-start | bytes 1216512 | tf_op jit(solution)/shard_map/all_gather | solution.py:52
  88.0 193.2 %all-gather.15.cloned.1.call-start = ((), (), s32[]{:S(2)}) async-start(), calls=%async_computation.10 | async-start | bytes 4866048 | tf_op jit(solution)/shard_map/all_gather | solution.py:56
  88.6 257.3 %all-gather.17.cloned.1.call-start = ((), (), s32[]{:S(2)}) async-start(), calls=%async_computation.11 | async-start | bytes 4866048 | tf_op jit(solution)/shard_map/all_gather | solution.py:58
  89.1 744.0 %reduce-scatter.19.cloned.1.call-start = ((), (), s32[]{:S(2)}) async-start(), calls=%async_computation.16 | async-start | bytes 5898240
  89.5 191.8 %copy-start.14 = (f32[768]{0:T(1024)}, f32[768]{0:T(1024)S(1)}, u32[]{:S(2)}) copy-start(f32[768]{0:T(1024)S(1)} %convert_element_type.159) | copy-start | bytes 9220
  253.1 1.0 copy-start.10
  253.1 3.5 copy-start
  259.5 116.2 %copy-start.2 = (f32[768,768]{1,0:T(8,128)}, f32[768,768]{1,0:T(8,128)S(1)}, u32[]{:S(2)}) copy-start(f32[768,768]{1,0:T(8,128)S(1)} %get-tuple-element.254) | copy-start | bytes 7077892
  259.9 0.9 copy-start.24
  260.8 85.0 %copy-start.6 = (bf16[2,384,768]{2,1,0:T(8,128)(2,1)S(1)}, bf16[2,384,768]{2,1,0:T(8,128)(2,1)}, u32[]{:S(2)}) copy-start(bf16[2,384,768]{2,1,0:T(8,128)(2,1)} %param.24) | copy-start | bytes 3538948
  345.9 29.9 %copy-start.31 = (bf16[768,3072]{1,0:T(8,128)(2,1)S(1)}, bf16[768,3072]{1,0:T(8,128)(2,1)}, u32[]{:S(2)}) copy-start(bf16[768,3072]{1,0:T(8,128)(2,1)} %all-gather.15.cloned.1.call-done) | copy-start | bytes 14155780
  375.7 4.8 copy-start.9
  375.7 4.8 copy-start.25
  383.1 2.0 copy-start.32
  383.2 3.2 copy-start.23
  384.2 1.0 copy-start.13
  756.1 74.5 %copy-start.4 = (bf16[12,2,384,64]{2,3,1,0:T(8,128)(2,1)}, bf16[12,2,384,64]{2,3,1,0:T(8,128)(2,1)S(1)}, u32[]{:S(2)}) copy-start(bf16[12,2,384,64]{2,3,1,0:T(8,128)(2,1)S(1)} %get-tuple-element.119) | copy-start | bytes 3538948
  774.3 97.0 %reduce-scatter.21.cloned.1.call-start = ((), (), s32[]{:S(2)}) async-start(), calls=%async_computation.17 | async-start | bytes 5898240
  792.8 4.2 copy-start.15
  792.8 185.0 %reduce-scatter.13.cloned.1.call-start = ((), (), s32[]{:S(2)}) async-start(), calls=%async_computation.13 | async-start | bytes 2433024 | tf_op jit(solution)/shard_map/reduce_scatter | solution.py:218
  797.0 321.6 %reduce-scatter.15.cloned.1.call-start = ((), (), s32[]{:S(2)}) async-start(), calls=%async_computation.14 | async-start | bytes 9732096 | tf_op jit(solution)/shard_map/reduce_scatter | solution.py:222
  807.9 0.7 copy-start.22
  808.0 452.2 %reduce-scatter.17.cloned.1.call-start = ((), (), s32[]{:S(2)}) async-start(), calls=%async_computation.15 | async-start | bytes 9732096 | tf_op jit(solution)/shard_map/reduce_scatter | solution.py:224
  830.3 554.5 %reduce-scatter.11.cloned.1.call-start = ((), (), s32[]{:S(2)}) async-start(), calls=%async_computation.12 | async-start | bytes 7299072 | tf_op jit(solution)/shard_map/reduce_scatter | solution.py:215
  874.2 7.3 copy-start.3
  877.5 5.1 copy-start.12
  889.8 0.7 copy-start.29
  889.8 2.8 copy-start.5
  902.8 7.2 copy-start.1
  902.8 7.2 copy-start.17
  902.8 7.2 copy-start.19
  910.1 7.2 copy-start.27
  910.1 8.6 copy-start.21
  917.2 1.4 copy-start.7
Sparse Core Ops, SparseCore 0:
  10.9 62.7 all-gather.6
  83.2 36.1 all-gather.8
  121.6 37.3 all-gather.10
  161.7 54.0 all-gather.12
  218.6 62.5 all-gather.14
  284.0 61.8 all-gather.16
  774.4 46.2 reduce-scatter.18
  823.3 47.9 reduce-scatter.20
  877.1 99.8 reduce-scatter.12
  983.3 135.2 reduce-scatter.14
  1125.1 135.0 reduce-scatter.16
  1266.3 118.3 reduce-scatter.10
where the time goes:
time: 1400 us; the launch traced here: 1390 us
  waiting for transfers between devices  591 us (42%)
  matrix products  489 us (35%)
  local copies, waits for them, and re-layouts  132 us (9%)
  blocking collectives  84.5 us (6%)
  other arithmetic  62.8 us (4%)
  loops' own time  16.1 us (1%)
  between operations  15.2 us (1%)
    reduce_scatter x1, waiting for transfers between devices, shards(): lax.psum_scatter(reduce_weight_grad, ('dp', 'seq'), scatter_dimension=0,...  142 us
    reduce_scatter x1, waiting for transfers between devices, shards(): lax.psum_scatter(expand_weight_grad, ('dp', 'seq'), scatter_dimension=0,...  141 us
    reduce_scatter x1, waiting for transfers between devices, shards(): lax.psum_scatter(proj_weight_grad, ('dp', 'seq'), scatter_dimension=0, ti...  125 us
    dot_general x12, matrix products, backward_head(): jnp.einsum('sqk,sqd->skd', score_grad, query_h, preferred_element_type=f32)  102 us
    dot_general x12, matrix products, backward_head(): jnp.einsum('sqk,skd->sqd', score_grad, keys_h, preferred_element_type=f32)  91.7 us
    unnamed x106, local copies, waits for them, and re-layouts  85.1 us
    unnamed x2, blocking collectives  84.5 us
    dot_general x24, matrix products, scores_of(): jnp.einsum('sqd,skd->sqk', query_h, keys_h, preferred_element_type=f32)  74.3 us
  transfers between devices with their start and end apart: 12, of which 9 were waited for; matrix products, arithmetic and copies ran while one was open for 18% of the time, Pallas kernels for 0%

commit v1 on v0

v1 whole, which is shorter than its diff:
```python
import functools

import jax
import jax.numpy as jnp
from jax import lax
from jax.experimental import pallas as pl
from jax.experimental.pallas import tpu as pltpu
from jax.sharding import PartitionSpec as P

HD = 64
LANES = 128
EPSILON = 1e-06
F32 = jnp.float32
BF16 = jnp.bfloat16
ALL = ("dp", "seq")


def head_lanes(rows, h):
    lane = lax.broadcasted_iota(jnp.int32, (rows, 128), 1)
    return (lane < 64) if h == 0 else (lane >= 64)

def fwd_kernel(tq, q_ref, k_ref, v_ref, bias_ref, o_ref, lse_ref):
    k = k_ref[...]
    v = v_ref[...]
    bias = bias_ref[...]
    def body(i, _):
        rows = pl.ds(pl.multiple_of(i * tq, tq), tq)
        q = q_ref[rows, :]
        outs = []
        for h in range(2):
            keep = head_lanes(tq, h)
            qh = jnp.where(keep, q, jnp.zeros_like(q))
            s = lax.dot_general(qh, k, (((1,), (1,)), ((), ())), preferred_element_type=F32) + bias
            top = jnp.max(s, axis=1, keepdims=True)
            e = jnp.exp(s - top)
            total = jnp.sum(e, axis=1, keepdims=True)
            o = jnp.dot(e.astype(BF16), v, preferred_element_type=F32) / total
            lse = top + jnp.log(total)
            lse_ref[0, h:h + 1, rows] = jnp.broadcast_to(lse, (tq, 128)).T[0:1, :]
            outs.append(o)
        o_ref[rows, :] = jnp.where(head_lanes(tq, 0), outs[0], outs[1]).astype(BF16)
        return 0
    lax.fori_loop(0, q_ref.shape[0] // tq, body, 0)

def attn_fwd(q, k, v, bias, tq=256):
    R, D = q.shape; K = k.shape[0]; P = D // 128
    return pl.pallas_call(
        functools.partial(fwd_kernel, tq),
        grid=(P,),
        in_specs=[pl.BlockSpec((R,128), lambda p:(0,p)), pl.BlockSpec((K,128), lambda p:(0,p)), pl.BlockSpec((K,128), lambda p:(0,p)), pl.BlockSpec((1,K), lambda p:(0,0))],
        out_specs=[pl.BlockSpec((R,128), lambda p:(0,p)), pl.BlockSpec((1,2,R), lambda p:(p,0,0))],
        out_shape=[jax.ShapeDtypeStruct((R,D),BF16), jax.ShapeDtypeStruct((P,2,R),F32)],
        compiler_params=pltpu.CompilerParams(vmem_limit_bytes=60<<20),
        name="attn_fwd",
    )(q,k,v,bias)

def bwd_kernel(tq, q_ref, k_ref, v_ref, g_ref, o_ref, lse_ref, bias_ref, dq_ref, dk_ref, dv_ref, dk_acc, dv_acc):
    k = k_ref[...]
    v = v_ref[...]
    K = k.shape[0]
    bias = bias_ref[...]
    dk_acc[...] = jnp.zeros_like(dk_acc)
    dv_acc[...] = jnp.zeros_like(dv_acc)
    def body(i, _):
        rows = pl.ds(pl.multiple_of(i * tq, tq), tq)
        q = q_ref[rows, :]
        g = g_ref[rows, :]
        go = g.astype(F32) * o_ref[rows, :].astype(F32)
        dq = None
        for h in range(2):
            keep = head_lanes(tq, h)
            qh = jnp.where(keep, q, jnp.zeros_like(q))
            gh = jnp.where(keep, g, jnp.zeros_like(g))
            delta = jnp.sum(jnp.where(keep, go, 0.0), axis=1, keepdims=True)
            delta = jnp.broadcast_to(delta, (tq, 128)).T[0:1, :]
            lse = lse_ref[0, h:h + 1, rows]
            s = lax.dot_general(k, qh, (((1,), (1,)), ((), ())), preferred_element_type=F32)
            p = jnp.exp(s + bias - lse)
            dp = lax.dot_general(v, gh, (((1,), (1,)), ((), ())), preferred_element_type=F32)
            ds = (p * (dp - delta)).astype(BF16)
            dv_acc[...] += jnp.dot(p.astype(BF16), gh, preferred_element_type=F32)
            dk_acc[...] += jnp.dot(ds, qh, preferred_element_type=F32)
            kh = jnp.where(head_lanes(K, h), k, jnp.zeros_like(k))
            part = lax.dot_general(ds, kh, (((0,), (0,)), ((), ())), preferred_element_type=F32)
            dq = part if dq is None else dq + part
        dq_ref[rows, :] = (dq * 0.125).astype(BF16)
        return 0
    lax.fori_loop(0, q_ref.shape[0] // tq, body, 0)
    dk_ref[...] = dk_acc[...].astype(BF16)
    dv_ref[...] = dv_acc[...].astype(BF16)

def attn_bwd(q, k, v, g, o, lse, bias_col, tq=256):
    R, D = q.shape; K = k.shape[0]; P = D // 128
    rs = pl.BlockSpec((R,128), lambda p:(0,p)); ks = pl.BlockSpec((K,128), lambda p:(0,p))
    return pl.pallas_call(
        functools.partial(bwd_kernel, tq),
        grid=(P,),
        in_specs=[rs, ks, ks, rs, rs, pl.BlockSpec((1,2,R), lambda p:(p,0,0)), pl.BlockSpec((K,1), lambda p:(0,0))],
        out_specs=[rs, ks, ks],
        out_shape=[jax.ShapeDtypeStruct((R,D),BF16), jax.ShapeDtypeStruct((K,D),BF16), jax.ShapeDtypeStruct((K,D),BF16)],
        scratch_shapes=[pltpu.VMEM((K,128),F32), pltpu.VMEM((K,128),F32)],
        compiler_params=pltpu.CompilerParams(vmem_limit_bytes=60<<20),
        name="attn_bwd",
    )(q,k,v,g,o,lse,bias_col)


def norm_rows(v, gain, shift):
    mean = jnp.mean(v, axis=-1, keepdims=True)
    center = v - mean
    spread = jnp.mean(center * center, axis=-1, keepdims=True)
    return center * lax.rsqrt(spread + EPSILON) * gain + shift


def gelu_exact(v):
    return jax.nn.gelu(v, approximate=False)


def shards(
    tokens,
    cube_lengths,
    key_mask,
    cotangent,
    norm_gain,
    norm_shift,
    proj_weight,
    query_bias,
    value_bias,
    merge_weight,
    merge_bias,
    mlp_gain,
    mlp_shift,
    expand_weight,
    expand_bias,
    reduce_weight,
    reduce_bias,
):
    slots, local_len, width = tokens.shape
    full_len = key_mask.shape[1]
    seq = full_len // local_len
    half = seq // slots
    rows = slots * local_len
    me = lax.axis_index("seq")
    cube = me // half

    across = [(i, (i + half) % seq) for i in range(seq)]
    around = [
        [(g * half + i, g * half + (i + r) % half) for g in range(slots) for i in range(half)]
        for r in range(half)
    ]

    def swap(pair):
        own = lax.dynamic_index_in_dim(pair, cube, 0, keepdims=False)
        other = lax.dynamic_index_in_dim(pair, 1 - cube, 0, keepdims=False)
        return own, lax.ppermute(other, "seq", across)

    def swap_back(own, other):
        back = lax.ppermute(other, "seq", across).astype(own.dtype)
        first = jnp.where(cube == 0, own, back)
        second = jnp.where(cube == 0, back, own)
        return jnp.stack([first, second])

    def gather(shard):
        return lax.all_gather(shard, ALL, axis=0, tiled=True)

    vectors = (
        norm_gain,
        norm_shift,
        query_bias,
        value_bias,
        merge_bias,
        mlp_gain,
        mlp_shift,
        reduce_bias,
        expand_bias,
    )
    packed_vectors = lax.all_gather(jnp.concatenate(vectors), ALL, axis=0)
    wide = []
    start = 0
    for vector in vectors:
        size = vector.shape[0]
        wide.append(packed_vectors[:, start : start + size].reshape(-1).astype(F32))
        start += size
    (
        gain_first,
        shift_first,
        query_add,
        value_add,
        merge_add,
        gain_second,
        shift_second,
        reduce_add,
        expand_add,
    ) = wide
    proj_full = gather(proj_weight)
    own_tokens, other_tokens = swap(tokens)
    own_cot, other_cot = swap(cotangent)
    resid = jnp.concatenate([own_tokens, other_tokens]).astype(F32)
    upstream = jnp.concatenate([own_cot, other_cot])
    merge_full = gather(merge_weight)
    expand_full = gather(expand_weight)
    reduce_full = gather(reduce_weight)

    length = lax.dynamic_index_in_dim(cube_lengths, cube, 0, keepdims=False)
    mask = lax.dynamic_index_in_dim(key_mask, cube, 0, keepdims=False)
    bias_all = jnp.where((mask > 0) & (jnp.arange(full_len) < length), 0.0, -1e30).astype(F32)
    blocks = []
    for r in range(half):
        device = cube * half + (me + half - r) % half
        for index in (device, (device + half) % seq):
            blocks.append(lax.dynamic_slice_in_dim(bias_all, index * local_len, local_len))
    bias = jnp.concatenate(blocks)

    first_f, first_pull = jax.vjp(norm_rows, resid, gain_first, shift_first)
    first = first_f.astype(BF16)
    packed = jnp.dot(first, proj_full, preferred_element_type=F32)
    query = (packed[:, :width] + query_add).astype(BF16)
    query = query * jnp.asarray(HD**-0.5, BF16)
    keys = packed[:, width : 2 * width].astype(BF16)
    values = (packed[:, 2 * width :] + value_add).astype(BF16)
    keys_all = jnp.concatenate([keys] + [lax.ppermute(keys, "seq", a) for a in around[1:]])
    values_all = jnp.concatenate([values] + [lax.ppermute(values, "seq", a) for a in around[1:]])
    attn, lse = attn_fwd(query, keys_all, values_all, bias[None, :])

    middle = resid + jnp.dot(attn, merge_full, preferred_element_type=F32) + merge_add
    second_f, second_pull = jax.vjp(norm_rows, middle, gain_second, shift_second)
    second = second_f.astype(BF16)
    hidden = jnp.dot(second, expand_full, preferred_element_type=F32) + expand_add
    act_f, gelu_pull = jax.vjp(gelu_exact, hidden)
    act = act_f.astype(BF16)
    output = middle + jnp.dot(act, reduce_full, preferred_element_type=F32) + reduce_add
    output = output.astype(BF16)
    activations = swap_back(output[:local_len], output[local_len:])

    def scatter(grad):
        return lax.psum_scatter(
            grad.astype(BF16), ALL, scatter_dimension=0, tiled=True
        ).astype(F32)

    upstream_f = upstream.astype(F32)
    reduce_bias_grad = jnp.sum(upstream_f, axis=0)
    reduce_weight_grad = scatter(
        jnp.einsum("rf,rd->fd", act, upstream, preferred_element_type=F32)
    )
    act_grad = jnp.einsum("rd,fd->rf", upstream, reduce_full, preferred_element_type=F32)
    hidden_grad = gelu_pull(act_grad)[0].astype(BF16)
    expand_bias_grad = jnp.sum(hidden_grad.astype(F32), axis=0)
    expand_weight_grad = scatter(
        jnp.einsum("rd,rf->df", second, hidden_grad, preferred_element_type=F32)
    )
    second_grad = jnp.einsum("rf,df->rd", hidden_grad, expand_full, preferred_element_type=F32)
    middle_norm, mlp_gain_grad, mlp_shift_grad = second_pull(second_grad)
    middle_grad = upstream_f + middle_norm
    merged_grad = middle_grad.astype(BF16)
    merge_bias_grad = jnp.sum(merged_grad.astype(F32), axis=0)
    merge_weight_grad = scatter(
        jnp.einsum("rd,re->de", attn, merged_grad, preferred_element_type=F32)
    )
    attn_grad = jnp.einsum("re,de->rd", merged_grad, merge_full, preferred_element_type=F32)
    attn_grad = attn_grad.astype(BF16)

    query_grad, key_parts, value_parts = attn_bwd(
        query, keys_all, values_all, attn_grad, attn, lse, bias[:, None]
    )

    def collect(parts):
        total = parts[:rows].astype(F32)
        for r in range(1, half):
            sent = parts[r * rows : (r + 1) * rows]
            back = [(j, i) for i, j in around[r]]
            total = total + lax.ppermute(sent, "seq", back).astype(F32)
        return total.astype(BF16)

    key_grad = collect(key_parts)
    value_grad = collect(value_parts)
    query_bias_grad = jnp.sum(query_grad.astype(F32), axis=0)
    value_bias_grad = jnp.sum(value_grad.astype(F32), axis=0)
    packed_grad = jnp.concatenate([query_grad, key_grad, value_grad], axis=1)
    proj_weight_grad = scatter(
        jnp.einsum("rd,re->de", first, packed_grad, preferred_element_type=F32)
    )
    first_grad = jnp.einsum("re,de->rd", packed_grad, proj_full, preferred_element_type=F32)
    resid_norm, norm_gain_grad, norm_shift_grad = first_pull(first_grad)
    input_sum = middle_grad + resid_norm
    input_grad = swap_back(input_sum[:local_len], input_sum[local_len:].astype(BF16))

    vector_grads = (
        norm_gain_grad,
        norm_shift_grad,
        query_bias_grad,
        value_bias_grad,
        merge_bias_grad,
        mlp_gain_grad,
        mlp_shift_grad,
        reduce_bias_grad,
        expand_bias_grad,
    )
    count = packed_vectors.shape[0]
    summed = lax.psum_scatter(
        jnp.concatenate([g.reshape(count, -1) for g in vector_grads], axis=1).reshape(-1),
        ALL,
        scatter_dimension=0,
        tiled=True,
    )
    small = []
    start = 0
    for vector in vectors:
        size = vector.shape[0]
        small.append(summed[start : start + size])
        start += size
    (
        norm_gain_grad,
        norm_shift_grad,
        query_bias_grad,
        value_bias_grad,
        merge_bias_grad,
        mlp_gain_grad,
        mlp_shift_grad,
        reduce_bias_grad,
        expand_bias_grad,
    ) = small
    return (
        activations,
        input_grad,
        norm_gain_grad,
        norm_shift_grad,
        proj_weight_grad,
        query_bias_grad,
        value_bias_grad,
        merge_weight_grad,
        merge_bias_grad,
        mlp_gain_grad,
        mlp_shift_grad,
        expand_weight_grad,
        expand_bias_grad,
        reduce_weight_grad,
        reduce_bias_grad,
    )


def solution(mesh):
    whole, part = P(ALL, None), P(ALL)
    block = P("dp", "seq", None)
    in_specs = (
        block,
        P("dp"),
        P("dp", None),
        block,
        part,
        part,
        whole,
        part,
        part,
        whole,
        part,
        part,
        part,
        whole,
        part,
        whole,
        part,
    )
    out_specs = (
        block,
        block,
        part,
        part,
        whole,
        part,
        part,
        whole,
        part,
        part,
        part,
        whole,
        part,
        whole,
        part,
    )
    return jax.shard_map(shards, mesh=mesh, in_specs=in_specs, out_specs=out_specs, check_vma=False)
```

time: 1400 us -> 801 us (0.57)
  matrix products: 489 us -> 105 us
  waiting for transfers between devices: 591 us -> 406 us
  local copies, waits for them, and re-layouts: 132 us -> 50.4 us
  Pallas kernels: 0 us -> 76.4 us
  other arithmetic: 62.8 us -> 39.7 us
  loops' own time: 16.1 us -> 0 us
    dot_general x96 -> x12, matrix products: 489 us -> 105 us  [the longest x1 29.2 us: shards(): jnp.dot(second, expand_full, preferred_element_type=F32) + expand_add]
    reduce_scatter x4, waiting for transfers between devices: 407 us -> 306 us  [scatter(): lax.psum_scatter(grad.astype(BF16), ALL, scatter_dimension=0, tiled=True)]
    pallas_call x0 -> x2, Pallas kernels: none -> 76.4 us  [the longest x1 45.7 us: attn_bwd(): pl.pallas_call(functools.partial(bwd_kernel, tq), grid=(P,), in_specs=[rs...]
    unnamed x106 -> x101, local copies, waits for them, and re-layouts: 85.1 us -> 9.34 us
    all_gather x6 -> x4, waiting for transfers between devices: 153 us -> 98.2 us  [gather(): return lax.all_gather(shard, ALL, axis=0, tiled=True)]
    unnamed x14 -> x8, waiting for transfers between devices: 31.7 us -> 2.14 us
    reduce_sum x15 -> x3, other arithmetic: 24.4 us -> 7.39 us  [the longest x1 2.79 us: shards(): value_bias_grad = jnp.sum(value_grad.astype(F32), axis=0)]
    another operation x2 -> x0, loops' own time: 16.1 us -> none  [the longest x1 8.13 us: shards(): lax.scan(backward_head, 0, (jnp.arange(heads), logsum))]
  transfers between devices with their start and end apart: 12 -> 16, of which waited for: 9 -> 6; matrix products, arithmetic and copies ran while one was open for 18% -> 18% of each run, Pallas kernels for 0% -> 4%
where the time goes in v1:
time: 801 us; the launch traced here: 791 us
  waiting for transfers between devices  406 us (51%)
  matrix products  105 us (13%)
  blocking collectives  89.3 us (11%)
  Pallas kernels  76.4 us (10%)
  local copies, waits for them, and re-layouts  50.4 us (6%)
  other arithmetic  39.7 us (5%)
  between operations  15.2 us (2%)
  starting transfers between devices  8.16 us (1%)
    reduce_scatter x4, waiting for transfers between devices, scatter(): lax.psum_scatter(grad.astype(BF16), ALL, scatter_dimension=0, tiled=True)  306 us
    all_gather x4, waiting for transfers between devices, gather(): return lax.all_gather(shard, ALL, axis=0, tiled=True)  98.2 us
    unnamed x2, blocking collectives  89.3 us
    pallas_call x1, Pallas kernels, attn_bwd(): pl.pallas_call(functools.partial(bwd_kernel, tq), grid=(P,), in_specs=[rs...  45.7 us
    pallas_call x1, Pallas kernels, attn_fwd(): pl.pallas_call(functools.partial(fwd_kernel, tq), grid=(P,), in_specs=[pl...  30.7 us
    dot_general x1, matrix products, shards(): jnp.dot(second, expand_full, preferred_element_type=F32) + expand_add  29.2 us
    dot_general x1, matrix products, shards(): jnp.einsum('rd,fd->rf', upstream, reduce_full, preferred_element_type=F32)  23.2 us
  transfers between devices with their start and end apart: 16, of which 6 were waited for; matrix products, arithmetic and copies ran while one was open for 18% of the time, Pallas kernels for 4%

profile of v1, /device:TPU:0, one launch (start us, length us, event | category | flops | bytes accessed | tf_op | source)
XLA Modules:
  0.0 790.7 jit_solution(3081708886298704137)
XLA Ops:
  9.5 2.8 constant_dynamic-slice_fusion
  12.6 3.1 collective-permute-start
  16.5 48.5 %all-reduce = bf16[9216]{0:T(1024)(128)(2,1)S(1)} all-reduce(bf16[9216]{0:T(1024)(128)(2,1)S(1)} %dynamic-update-slice), channel_id=2, replica_groups=mesh['dp'=8,'seq'=4] {'dp','seq'}, use_global_device_ids=true, to_apply=%add | all-reduce | flops 9216 | bytes 36864
  67.4 7.3 all-gather.6.cloned.1.call-done
  74.8 5.1 fusion.34
  80.6 1.3 fusion.40
  82.1 2.2 copy.59
  84.3 1.5 collective-permute-start.4
  85.8 1.2 dynamic_slice.36
  89.1 1.2 broadcast_in_dim.47.bias_ref
  90.3 1.4 reshape.212
  91.7 1.4 reshape.213
  93.1 1.4 reshape.214
  94.5 1.4 slice_convert_fusion.3
  95.9 1.4 reshape.215
  97.2 2.2 copy.58
  99.4 2.8 pad_maximum_fusion.2.v_ref
  102.2 2.8 pad_maximum_fusion.1.k_ref
  105.0 30.7 %attn_fwd.1 = (bf16[768,768]{1,0:T(8,128)(2,1)}, f32[6,2,768]{2,1,0:T(2,128)}) custom-call(bf16[768,768]{1,0:T(8,128)(2,1)} %get-tuple-element.83.q_ref, bf16[1536,768]{1,0:T(8,128)(2,1)} %pad_maximum_fusion.1.k_ref, bf16[1536,768]{1,0:T(8,128)(2,1)} %pad_maximum_fusion.2.v_ref, f32[1,1536]{1,0:T(1,128)} %broadcast_in_dim.22.bias_ref), custom_call_target="tpu_custom_call" | custom-call | tf_op jit(solution)/shard_map/attn_fwd/pallas_call | solution.py:47
  135.7 2.8 fusion.43
  140.6 55.3 %all-gather.10.cloned.1.call-done = bf16[768,3072]{1,0:T(8,128)(2,1)} async-done(((bf16[24,3072]{1,0:T(8,128)(2,1)}), bf16[768,3072]{1,0:T(8,128)(2,1)}) %all-gather.10.cloned.1.call-update) | async-done | bytes 4718608 | tf_op jit(solution)/shard_map/all_gather | solution.py:163
  195.9 29.2 %multiply_convert_fusion = (bf16[768,3072]{1,0:T(8,128)(2,1)}, f32[768,3072]{1,0:T(8,128)}, f32[768,3072]{1,0:T(8,128)}) fusion(f32[3072]{0:T(1024)} %reshape.215, bf16[768,3072]{1,0:T(8,128)(2,1)} %all-gather.10.cloned.1.call-done, f32[768,768]{0,1:T(8,128)S(1)} %get-tuple-element.115, f32[768]{0:T(1024)} %reshape.214, f32[768]{0:T(1024)} %reshape.213, ...), kind=kOutput, calls=%fused_computation.4 | convolution fusion | flops 3782541312 | bytes 30695424 | tf_op jit(solution)/shard_map/dot_general | solution.py:227
  225.1 35.5 %all-gather.12.cloned.1.call-done = bf16[3072,768]{1,0:T(8,128)(2,1)} async-done(((bf16[96,768]{1,0:T(8,128)(2,1)}), bf16[3072,768]{1,0:T(8,128)(2,1)}) %all-gather.12.cloned.1.call-update) | async-done | bytes 4718608 | tf_op jit(solution)/shard_map/all_gather | solution.py:163
  260.6 23.2 %convert_reduce_fusion = (f32[3072]{0:T(1024)}, bf16[768,3072]{1,0:T(8,128)(2,1)S(1)}) fusion(f32[768,3072]{1,0:T(8,128)} %get-tuple-element.81, bf16[3072,768]{1,0:T(8,128)(2,1)} %all-gather.12.cloned.1.call-done, bf16[384,768]{0,1:T(8,128)(2,1)} %collective-permute-done.4, bf16[384,768]{0,1:T(8,128)(2,1)} %bitcast.37, f32[768,3072]{1,0:T(8,128)} %get-tuple-element.116, ...), kind=kOutput, calls=%fused_computation.2 | convolution fusion | flops 3666342912 | bytes 29515776 | tf_op jit(solution)/shard_map/rd,fd->rf/dot_general | solution.py:244
  283.8 5.9 fusion.45
  289.7 3.1 copy.60
  292.8 3.1 multiply_reduce_fusion
  297.0 2.5 convert_reduce_fusion.3
  299.6 2.2 convolution_convert_fusion.4.g_ref
  301.7 45.7 %attn_bwd.1 = (bf16[768,768]{1,0:T(8,128)(2,1)}, bf16[1536,768]{1,0:T(8,128)(2,1)}, bf16[1536,768]{1,0:T(8,128)(2,1)}) custom-call(bf16[768,768]{1,0:T(8,128)(2,1)} %get-tuple-element.83.q_ref, bf16[1536,768]{1,0:T(8,128)(2,1)} %pad_maximum_fusion.1.k_ref, bf16[1536,768]{1,0:T(8,128)(2,1)} %pad_maximum_fusion.2.v_ref, ...), custom_call_target="tpu_custom_call" | custom-call | tf_op jit(solution)/shard_map/attn_bwd/pallas_call | solution.py:95
  347.5 2.5 slice.104
  350.3 1.1 slice.106
  351.6 2.2 convolution_convert_fusion.3
  353.9 2.1 add_convert_fusion.2
  356.3 2.8 convert_reduce_fusion.4
  359.1 1.0 copy-done.16
  360.1 5.0 convolution_convert_fusion
  365.8 8.1 %convolution_convert_fusion.2 = bf16[768,3072]{1,0:T(8,128)(2,1)} fusion(bf16[768,3072]{1,0:T(8,128)(2,1)} %copy-done.47, f32[768,768]{0,1:T(8,128)S(1)} %get-tuple-element.115, f32[768]{0:T(1024)} %reshape.214, f32[768]{0:T(1024)} %reshape.213, f32[768]{0:T(1024)} %fusion.29, f32[768]{0:T(1024)S(1)} %copy-done.25), kind=kOutput, calls=%fused_computation.20 | convolution fusion | flops 3629187072 | bytes 11808768 | tf_op jit(solution)/shard_map/rd,rf->df/dot_general | solution.py:248
  374.2 8.8 %convolution_convert_fusion.1 = bf16[3072,768]{1,0:T(8,128)(2,1)} fusion(bf16[768,3072]{1,0:T(8,128)(2,1)} %get-tuple-element.80, bf16[384,768]{0,1:T(8,128)(2,1)} %collective-permute-done.4, bf16[384,768]{0,1:T(8,128)(2,1)} %bitcast.38), kind=kOutput, calls=%fused_computation.19 | convolution fusion | flops 3628597248 | bytes 10616832 | tf_op jit(solution)/shard_map/rf,rd->fd/dot_general | solution.py:242
  383.0 1.4 reshape.216
  384.4 2.1 convert_reduce_fusion.5
  386.5 1.4 reshape.200
  388.6 1.4 reshape.203
  390.0 1.4 reshape.204
  391.3 1.4 reshape.206
  392.7 7.8 add_convert_fusion.3
  401.5 1.5 collective-permute-start.3
  403.0 4.9 fusion.44
  407.9 2.3 copy.62
  410.9 1.6 fusion.14
  412.7 3.1 convert_reduce_fusion.2
  415.8 1.4 copy-done.3
  418.7 1.2 select_bitcast_fusion.1
  420.1 1.5 copy.65
  425.6 40.8 %all-reduce.1 = f32[9216]{0:T(1024)S(1)} all-reduce(f32[9216]{0:T(1024)S(1)} %reshape.207), channel_id=3, replica_groups=mesh['dp'=8,'seq'=4] {'dp','seq'}, use_global_device_ids=true, to_apply=%region_17.18.clone | all-reduce | flops 9216 | bytes 73728
  467.6 1.4 convert_element_type.225
  469.1 1.2 fusion.22
  470.6 1.9 copy.66
  472.5 85.3 %reduce-scatter.5.cloned.1.call-done = bf16[24,2304]{1,0:T(8,128)(2,1)} async-done(((bf16[768,2304]{1,0:T(8,128)(2,1)}), bf16[24,2304]{1,0:T(8,128)(2,1)}) %reduce-scatter.5.cloned.1.call-update) | async-done | bytes 110608 | tf_op jit(solution)/shard_map/reduce_scatter | solution.py:235
  557.9 1.6 convert_element_type.223
  559.5 110.4 %reduce-scatter.9.cloned.1.call-done = bf16[24,3072]{1,0:T(8,128)(2,1)} async-done(((bf16[768,3072]{1,0:T(8,128)(2,1)}), bf16[24,3072]{1,0:T(8,128)(2,1)}) %reduce-scatter.9.cloned.1.call-update) | async-done | bytes 147472 | tf_op jit(solution)/shard_map/reduce_scatter | solution.py:235
  669.9 1.6 convert_element_type.227
  671.5 110.3 %reduce-scatter.11.cloned.1.call-done = bf16[96,768]{1,0:T(8,128)(2,1)} async-done(((bf16[3072,768]{1,0:T(8,128)(2,1)}), bf16[96,768]{1,0:T(8,128)(2,1)}) %reduce-scatter.11.cloned.1.call-update) | async-done | bytes 147472 | tf_op jit(solution)/shard_map/reduce_scatter | solution.py:235
  781.8 1.6 convert_element_type.229
  (169 shorter events, 23.3 us)
Async XLA Ops:
  7.2 67.6 %all-gather.6.cloned.1.call-start = ((), (), s32[]{:S(2)}) async-start(), calls=%async_computation.4 | async-start | bytes 3649536 | tf_op jit(solution)/shard_map/all_gather | solution.py:163
  7.9 127.8 %all-gather.8.cloned.1.call-start = ((), (), s32[]{:S(2)}) async-start(), calls=%async_computation.5 | async-start | bytes 1216512 | tf_op jit(solution)/shard_map/all_gather | solution.py:163
  8.7 187.3 %all-gather.10.cloned.1.call-start = ((), (), s32[]{:S(2)}) async-start(), calls=%async_computation.6 | async-start | bytes 4866048 | tf_op jit(solution)/shard_map/all_gather | solution.py:163
  9.4 251.2 %all-gather.12.cloned.1.call-start = ((), (), s32[]{:S(2)}) async-start(), calls=%async_computation.7 | async-start | bytes 4866048 | tf_op jit(solution)/shard_map/all_gather | solution.py:163
  12.2 3.8 copy-start.36
  12.3 3.9 copy-start.37
  12.3 3.9 copy-start.38
  12.3 3.9 copy-start.39
  12.3 3.9 copy-start.40
  12.3 3.9 copy-start.41
  12.3 3.9 copy-start.42
  12.3 3.9 copy-start.43
  12.3 3.9 copy-start.44
  12.6 54.2 %collective-permute-start = (bf16[384,768]{0,1:T(8,128)(2,1)S(1)}, bf16[384,768]{0,1:T(8,128)(2,1)S(1)}, u32[]{:S(2)}, u32[]{:S(2)}) collective-permute-start(bf16[384,768]{0,1:T(8,128)(2,1)S(1)} %bitcast.42), channel_id=1, source_target_pairs={{0,2},{1,3},{2,0},{3,1},{4,6},{5,7},{6,4},{7,5},{8,10},{9,11},{10,... | collective-permute-start | bytes 1769480 | tf_op jit(solution)/shard_map/ppermute | solution.py:154
  15.7 451.9 %reduce-scatter.7.cloned.1.call-start = ((), (), s32[]{:S(2)}) async-start(), calls=%async_computation.9 | async-start | bytes 1216512 | tf_op jit(solution)/shard_map/reduce_scatter | solution.py:235
  65.1 14.7 %copy-start.21 = (bf16[32,288]{1,0:T(8,128)(2,1)}, bf16[32,288]{1,0:T(8,128)(2,1)S(1)}, u32[]{:S(2)}) copy-start(bf16[32,288]{1,0:T(8,128)(2,1)S(1)} %reshape.217) | copy-start | bytes 55300
  67.4 12.5 %copy-start.28 = (f32[768]{0:T(1024)}, f32[768]{0:T(1024)S(1)}, u32[]{:S(2)}) copy-start(f32[768]{0:T(1024)S(1)} %fusion.15) | copy-start | bytes 9220
  79.9 0.7 copy-start.35
  80.1 19.3 %collective-permute-start.2 = (bf16[768,768]{1,0:T(8,128)(2,1)S(1)}, bf16[768,768]{1,0:T(8,128)(2,1)}, u32[]{:S(2)}, u32[]{:S(2)}) collective-permute-start(bf16[768,768]{1,0:T(8,128)(2,1)S(1)} %fusion.18), channel_id=1, source_target_pairs={{0,1},{1,0},{2,3},{3,2},{4,5},{5,4},{6,7},{7,6},{8,9},{9,8},{10,11... | collective-permute-start | bytes 3538952 | tf_op jit(solution)/shard_map/ppermute | solution.py:221
  81.9 20.3 %collective-permute-start.1 = (bf16[768,768]{1,0:T(8,128)(2,1)S(1)}, bf16[768,768]{1,0:T(8,128)(2,1)}, u32[]{:S(2)}, u32[]{:S(2)}) collective-permute-start(bf16[768,768]{1,0:T(8,128)(2,1)S(1)} %get-tuple-element.82), channel_id=1, source_target_pairs={{0,1},{1,0},{2,3},{3,2},{4,5},{5,4},{6,7},{7,6},{8,9},{9,8},{10,11... | collective-permute-start | bytes 3538952 | tf_op jit(solution)/shard_map/ppermute | solution.py:220
  84.3 140.8 %collective-permute-start.4 = (bf16[384,768]{0,1:T(8,128)(2,1)}, bf16[384,768]{0,1:T(8,128)(2,1)}, u32[]{:S(2)}, u32[]{:S(2)}) collective-permute-start(bf16[384,768]{0,1:T(8,128)(2,1)} %bitcast.41), channel_id=1, source_target_pairs={{0,2},{1,3},{2,0},{3,1},{4,6},{5,7},{6,4},{7,5},{8,10},{9,11},{10,... | collective-permute-start | bytes 1769480 | tf_op jit(solution)/shard_map/ppermute | solution.py:154
  138.5 0.6 copy-start.23
  139.4 0.6 copy-start.30
  260.6 23.2 %copy-start.45 = (bf16[768,3072]{1,0:T(8,128)(2,1)S(1)}, bf16[768,3072]{1,0:T(8,128)(2,1)}, u32[]{:S(2)}) copy-start(bf16[768,3072]{1,0:T(8,128)(2,1)} %all-gather.10.cloned.1.call-done) | copy-start | bytes 14155780
  283.8 5.9 copy-start.47
  292.7 3.2 copy-start.31
  292.8 3.2 copy-start.2
  292.8 3.2 copy-start.24
  292.8 3.2 copy-start.32
  292.8 3.2 copy-start.33
  296.0 1.1 copy-start.5
  296.6 3.0 copy-start
  296.6 2.9 copy-start.26
  297.0 2.5 copy-start.46
  299.6 2.2 copy-start.19
  347.5 2.8 copy-start.8
  347.5 4.1 copy-start.18
  347.5 4.1 copy-start.20
  350.0 3.9 collective-permute-start.5
  351.3 4.6 collective-permute-start.6
  353.8 204.1 %reduce-scatter.5.cloned.1.call-start = ((), (), s32[]{:S(2)}) async-start(), calls=%async_computation.8 | async-start | bytes 3649536 | tf_op jit(solution)/shard_map/reduce_scatter | solution.py:235
  353.9 2.4 copy-start.9
  356.0 3.1 copy-start.10
  356.0 4.1 copy-start.14
  359.0 1.0 copy-start.16
  365.1 0.7 copy-start.25
  365.1 304.8 %reduce-scatter.9.cloned.1.call-start = ((), (), s32[]{:S(2)}) async-start(), calls=%async_computation.10 | async-start | bytes 4866048 | tf_op jit(solution)/shard_map/reduce_scatter | solution.py:235
  373.9 407.9 %reduce-scatter.11.cloned.1.call-start = ((), (), s32[]{:S(2)}) async-start(), calls=%async_computation.11 | async-start | bytes 4866048 | tf_op jit(solution)/shard_map/reduce_scatter | solution.py:235
  383.0 4.9 copy-start.34
  392.7 10.3 %copy-start.7 = (bf16[768,2304]{1,0:T(8,128)(2,1)S(1)}, bf16[768,2304]{1,0:T(8,128)(2,1)}, u32[]{:S(2)}) copy-start(bf16[768,2304]{1,0:T(8,128)(2,1)} %all-gather.6.cloned.1.call-done) | copy-start | bytes 10616836
  392.7 10.3 %copy-start.11 = (bf16[768,768]{1,0:T(8,128)(2,1)S(1)}, bf16[768,768]{1,0:T(8,128)(2,1)}, u32[]{:S(2)}) copy-start(bf16[768,768]{1,0:T(8,128)(2,1)} %copy-done.10) | copy-start | bytes 3538948
  392.7 10.3 %copy-start.15 = (bf16[768,768]{1,0:T(8,128)(2,1)S(1)}, bf16[768,768]{1,0:T(8,128)(2,1)}, u32[]{:S(2)}) copy-start(bf16[768,768]{1,0:T(8,128)(2,1)} %get-tuple-element.22) | copy-start | bytes 3538948
  392.7 10.3 %copy-start.17 = (bf16[768,768]{1,0:T(8,128)(2,1)S(1)}, bf16[768,768]{1,0:T(8,128)(2,1)}, u32[]{:S(2)}) copy-start(bf16[768,768]{1,0:T(8,128)(2,1)} %copy-done.16) | copy-start | bytes 3538948
  400.6 7.4 copy-start.12
  401.5 17.2 %collective-permute-start.3 = (bf16[384,768]{0,1:T(8,128)(2,1)}, bf16[384,768]{0,1:T(8,128)(2,1)}, u32[]{:S(2)}, u32[]{:S(2)}) collective-permute-start(bf16[384,768]{0,1:T(8,128)(2,1)} %slice.131), channel_id=1, source_target_pairs={{0,2},{1,3},{2,0},{3,1},{4,6},{5,7},{6,4},{7,5},{8,10},{9,11},{10,... | collective-permute-start | bytes 1769480 | tf_op jit(solution)/shard_map/ppermute | solution.py:157
  410.2 0.7 copy-start.29
  410.9 1.7 copy-start.1
  410.9 1.8 copy-start.6
  410.9 1.8 copy-start.27
  412.7 6.0 copy-start.13
  415.8 1.4 copy-start.3
  418.1 50.9 %collective-permute-start.7 = (bf16[384,768]{0,1:T(8,128)(2,1)}, bf16[384,768]{0,1:T(8,128)(2,1)}, u32[]{:S(2)}, u32[]{:S(2)}) collective-permute-start(bf16[384,768]{0,1:T(8,128)(2,1)} %slice.160), channel_id=1, source_target_pairs={{0,2},{1,3},{2,0},{3,1},{4,6},{5,7},{6,4},{7,5},{8,10},{9,11},{10,... | collective-permute-start | bytes 1769480 | tf_op jit(solution)/shard_map/ppermute | solution.py:157
  419.9 4.7 copy-start.22
  419.9 49.1 %copy-start.4 = (f32[768,768]{0,1:T(8,128)S(1)}, f32[768,768]{0,1:T(8,128)}, u32[]{:S(2)}) copy-start(f32[768,768]{0,1:T(8,128)} %copy-done.3) | copy-start | bytes 7077892
Sparse Core Ops, SparseCore 0:
  10.9 63.8 all-gather.5
  77.7 52.8 all-gather.7
  133.4 62.4 all-gather.9
  198.7 61.8 all-gather.11
  353.9 96.1 reduce-scatter.6
  455.4 102.4 reduce-scatter.4
  563.4 106.4 reduce-scatter.8
  675.3 106.4 reduce-scatter.10
